TPU v7x, 256 devices: a whole 4x4x8 slice. The times are simulated.
256 devices in a mesh: member: 16 (over x, z_lo), band: 16 (over z_hi, y, core).
Axes of the slice: x: 4, y: 4, z: 8 (z_hi: 2, z_lo: 4; z = z_hi * 4 + z_lo), core: 2. Of those that a mesh axis runs over, the one named last changes fastest.
Arguments:
- prior: bfloat16 [16, 2, 768, 1536], P('member', None, 'band'), may hold values from -9 to 9
- analysis: bfloat16 [16, 2, 768, 1536], P('member', None, 'band'), may hold values from -6 to 6
- increment: float32 [2, 768, 1536], P(None, 'band'), may hold values from -6 to 6
- truncation: int32 [2], replicated, may hold values from 128 to 511
Outputs:
- members: bfloat16 [16, 2, 768, 1536], P('member', None, 'band')
All inputs are finite; a program needn't handle non-finite values.
Results may differ from a plain program's by a relative error of at most 0.001.
Values sent between devices are 32-bit elements; how exact they have to be, the bound alone decides.
A program may use at most 64 MiB of HBM per device.

v0:
```python
import math

import jax
import jax.numpy as jnp
from jax import lax
from jax.sharding import PartitionSpec as P

MW = 512


RELAX = 0.85
SPREAD_FLOOR = 0.25


def laid_out(tiles, dim):
    lengths = list(tiles.shape[1:])
    lengths[dim] *= tiles.shape[0]
    return jnp.moveaxis(tiles, 0, dim).reshape(lengths)


def copy_for_each(array, axis):
    size = lax.axis_size(axis)
    return lax.all_to_all(
        jnp.broadcast_to(array[None], (size, *array.shape)), axis, 0, 0, tiled=True
    )


def gather_directly(array, axis, dim):
    return laid_out(copy_for_each(array, axis), dim)


def zonal_table(nlon, waves):
    column = jnp.arange(nlon, dtype=jnp.int32)[:, None]
    number = jnp.arange(waves, dtype=jnp.int32)[None, :]
    phase = (column * number % nlon).astype(jnp.float32) * (2.0 * math.pi / nlon)
    return jnp.stack([jnp.cos(phase), jnp.sin(phase)], axis=2).reshape(nlon, 2 * waves)


def cosine_table(nlat):
    order = jnp.arange(nlat, dtype=jnp.int32)[:, None]
    place = jnp.arange(nlat, dtype=jnp.int32)[None, :]
    phase = ((2 * place + 1) * order % (4 * nlat)).astype(jnp.float32) * (math.pi / (2.0 * nlat))
    scale = jnp.where(
        order == 0, jnp.float32(math.sqrt(1.0 / nlat)), jnp.float32(math.sqrt(2.0 / nlat))
    )
    return scale * jnp.cos(phase)


def column_weights(waves, nlon):
    number = jnp.arange(2 * waves, dtype=jnp.int32) // 2
    return jnp.where(number == 0, jnp.float32(1.0 / nlon), jnp.float32(2.0 / nlon))


def inflation(sums, count):
    mean_b = sums[0] / count
    mean_a = sums[2] / count
    spread_b = jnp.sqrt(jnp.maximum((sums[1] - count * mean_b * mean_b) / (count - 1), 0.0))
    spread_a = jnp.maximum(
        jnp.sqrt(jnp.maximum((sums[3] - count * mean_a * mean_a) / (count - 1), 0.0)), SPREAD_FLOOR
    )
    factor = 1.0 + RELAX * (spread_b - spread_a) / spread_a
    return (factor, mean_b - factor * mean_a)


def truncated(increment, truncation):
    levels, lat_rows, nlon = increment.shape
    table = zonal_table(nlon, MW)
    coef = jnp.dot(
        increment.reshape(levels * lat_rows, nlon), table, precision=lax.Precision.HIGHEST
    ).reshape(levels, lat_rows, 2 * MW)
    waves = lax.all_to_all(coef, "band", split_axis=2, concat_axis=1, tiled=True)
    nlat = waves.shape[1]
    width = waves.shape[2]
    cosines = cosine_table(nlat)
    spec = jnp.einsum("ki,lim->lkm", cosines, waves, precision=lax.Precision.HIGHEST)
    order = jnp.arange(nlat, dtype=jnp.int32)[:, None]
    number = ((lax.axis_index("band") * width + jnp.arange(width, dtype=jnp.int32)) // 2)[None, :]
    keep = (order * order + number * number)[None] <= (truncation * truncation)[:, None, None]
    kept = jnp.einsum(
        "ki,lkm->lim", cosines, jnp.where(keep, spec, 0.0), precision=lax.Precision.HIGHEST
    )
    rows = lax.all_to_all(kept, "band", split_axis=1, concat_axis=2, tiled=True)
    weighted = rows * column_weights(MW, nlon)
    return jnp.dot(
        weighted.reshape(levels * lat_rows, 2 * MW), table.T, precision=lax.Precision.HIGHEST
    ).reshape(levels, lat_rows, nlon)


def on_device(prior, analysis, increment, truncation):
    count = prior.shape[0] * lax.axis_size("member")
    a_vals = analysis.astype(jnp.float32)
    b_vals = prior.astype(jnp.float32)
    terms = jnp.stack(
        [
            jnp.sum(b_vals, 0),
            jnp.sum(b_vals * b_vals, 0),
            jnp.sum(a_vals, 0),
            jnp.sum(a_vals * a_vals, 0),
        ]
    )
    portion = lax.psum_scatter(terms, "member", scatter_dimension=3, tiled=True)
    factor, shift = inflation(portion, count)
    joined = gather_directly(jnp.stack([factor, shift]), "member", 3)
    factor = joined[0]
    shift = joined[1]
    smooth = truncated(increment, truncation)
    return ((shift + smooth)[None] + factor[None] * a_vals).astype(jnp.bfloat16)


def solution(mesh):
    placed = (
        P("member", None, "band", None),
        P("member", None, "band", None),
        P(None, "band", None),
        P(),
    )
    return jax.shard_map(
        on_device,
        mesh=mesh,
        in_specs=placed,
        out_specs=P("member", None, "band", None),
        check_vma=False,
    )
```

profile of v0, /device:TPU:8, one launch (start us, length us, event | category | flops | bytes accessed | tf_op | source)
XLA Modules:
  0.0 220.0 jit_solution(8589760159528115499)
XLA Ops:
  9.0 6.5 %copy.34 = f32[4,2,48,1536]{2,1,0,3:T(2,128)} copy(f32[4,2,48,1536]{3,2,1,0:T(8,128)S(1)} %pad_maximum_fusion.1) | data formatting | bytes 4718592
  15.5 10.5 %reshape.182 = f32[1536,384]{1,0:T(8,128)} reshape(f32[1536,4,2,48]{3,2,1,0:T(2,128)} %bitcast.70) | data formatting | bytes 4718592
  26.1 12.9 %fusion.6 = (f32[1536,512,1]{1,0,2:T(8,128)S(1)}, f32[1536,512,1]{1,0,2:T(8,128)S(1)}) fusion(), kind=kLoop, calls=%fused_computation.10 | loop fusion | flops 7077888 | bytes 6291456 | tf_op jit(solution)/shard_map/sin | solution.py:36
  38.9 3.4 %pad_maximum_fusion = f32[1536,512,2]{1,0,2:T(8,128)} fusion(f32[1536,512,1]{1,0,2:T(8,128)S(1)} %get-tuple-element.15, f32[1536,512,1]{1,0,2:T(8,128)S(1)} %get-tuple-element.16), kind=kLoop, calls=%fused_computation | loop fusion | flops 1572864 | bytes 12582912 | tf_op jit(solution)/shard_map/stack | solution.py:36
  42.3 10.4 %copy.20 = f32[1536,512,2]{0,2,1:T(2,128)} copy(f32[1536,512,2]{1,0,2:T(8,128)} %pad_maximum_fusion) | data formatting | bytes 12582912 | tf_op jit(solution)/shard_map/stack | solution.py:36
  52.7 8.5 %reshape.177 = f32[1536,1024]{0,1:T(8,128)} reshape(f32[1536,512,2]{0,2,1:T(2,128)} %copy.20) | data formatting | bytes 12582912 | tf_op jit(solution)/shard_map/reshape | solution.py:36
  61.2 8.3 %fusion.79 = f32[1024,96]{0,1:T(8,128)S(1)} fusion(f32[1536,1024]{0,1:T(8,128)} %reshape.177, f32[96,1536]{1,0:T(8,128)S(1)} %bitcast.69), kind=kOutput, calls=%fused_computation.87 | convolution fusion | flops 1811939328 | bytes 7274496 | tf_op jit(solution)/shard_map/dot_general | solution.py:68
  70.1 2.6 %reshape.184 = f32[16,1,6144]{2,1,0:T(1,128)} reshape(f32[1024,2,48]{2,1,0:T(2,128)S(1)} %bitcast.72) | data formatting | bytes 786432
  72.6 11.9 %all-to-all-start.1 = ((f32[16,1,6144]{2,1,0:T(1,128)}), f32[16,1,6144]{2,1,0:T(1,128)S(1)}, u32[]{:S(2)}, u32[]{:S(2)}) async-start(f32[16,1,6144]{2,1,0:T(1,128)} %reshape.184), calls=%async_computation.1 | async-start | bytes 786432 | tf_op jit(solution)/shard_map/all_to_all | solution.py:71
  85.4 13.2 %all-to-all-done.1 = f32[16,1,6144]{2,1,0:T(1,128)S(1)} async-done(((f32[16,1,6144]{2,1,0:T(1,128)}), f32[16,1,6144]{2,1,0:T(1,128)S(1)}, u32[]{:S(2)}, u32[]{:S(2)}) %all-to-all-start.1) | async-done | bytes 393248 | tf_op jit(solution)/shard_map/all_to_all | solution.py:71
  99.3 1.6 reduce
  100.9 1.7 reshape.185
  103.6 12.0 %fusion.49 = f32[2,768,64]{1,2,0:T(8,128)S(1)} fusion(f32[2,768,64]{1,2,0:T(8,128)S(1)} %all_to_all.29, s32[768]{0:T(1024)S(1)} %multiply_add_fusion.1, f32[768]{0:T(1024)S(1)} %fusion.68, s32[768,64]{0,1:T(8,128)} %broadcast_add_fusion, s32[2]{0:T(128)S(1)} %mul.189), kind=kOutput, calls=%fused_computation.39 | convolution fusion | flops 912064512 | bytes 989192 | tf_op jit(solution)/shard_map/ki,lim->lkm/dot_general | solution.py:75
  115.7 10.6 %fusion.36 = f32[2,768,64]{1,2,0:T(8,128)S(1)} fusion(f32[2,768,64]{1,2,0:T(8,128)S(1)} %fusion.49, s32[768]{0:T(1024)S(1)} %multiply_add_fusion.1, f32[768]{0:T(1024)S(1)} %fusion.68), kind=kOutput, calls=%fused_computation.30 | convolution fusion | flops 911867904 | bytes 792576 | tf_op jit(solution)/shard_map/ki,lkm->lim/dot_general | solution.py:79
  126.7 1.6 reshape.186
  128.3 8.7 %all-to-all-start.2 = ((f32[16,1,6144]{2,1,0:T(1,128)}), f32[16,1,6144]{2,1,0:T(1,128)S(1)}, u32[]{:S(2)}, u32[]{:S(2)}) async-start(f32[16,1,6144]{2,1,0:T(1,128)} %reshape.186), calls=%async_computation.2 | async-start | bytes 786432 | tf_op jit(solution)/shard_map/all_to_all | solution.py:82
  136.9 1.5 reshape.183
  139.1 8.0 %all-to-all-done.2 = f32[16,1,6144]{2,1,0:T(1,128)S(1)} async-done(((f32[16,1,6144]{2,1,0:T(1,128)}), f32[16,1,6144]{2,1,0:T(1,128)S(1)}, u32[]{:S(2)}, u32[]{:S(2)}) %all-to-all-start.2) | async-done | bytes 393248 | tf_op jit(solution)/shard_map/all_to_all | solution.py:82
  148.4 11.5 %all-to-all-start = ((f32[16,2,2,48,96]{4,3,2,1,0:T(8,128)}), f32[16,2,2,48,96]{4,3,2,1,0:T(8,128)S(1)}, u32[]{:S(2)}, u32[]{:S(2)}) async-start(f32[16,2,2,48,96]{4,3,2,1,0:T(8,128)} %broadcast_in_dim.38), calls=%async_computation | async-start | bytes 3145728 | tf_op jit(solution)/shard_map/all_to_all | solution.py:23
  159.9 1.6 reduce.1
  161.6 1.5 reshape.187
  165.9 1.8 copy.26
  168.7 35.1 %all-to-all-done = f32[16,2,2,48,96]{4,3,2,1,0:T(8,128)S(1)} async-done(((f32[16,2,2,48,96]{4,3,2,1,0:T(8,128)}), f32[16,2,2,48,96]{4,3,2,1,0:T(8,128)S(1)}, u32[]{:S(2)}, u32[]{:S(2)}) %all-to-all-start) | async-done | bytes 1179680 | tf_op jit(solution)/shard_map/all_to_all | solution.py:23
  205.6 7.4 %fusion.30 = bf16[1,2,48,1536]{3,2,1,0:T(8,128)(2,1)} fusion(f32[2,48,1536]{2,1,0:T(8,128)S(1)} %squeeze.2, f32[2,48,1024]{2,1,0:T(8,128)} %mul.207, f32[1536,1024]{0,1:T(8,128)} %reshape.177, f32[1,2,48,1536]{3,2,1,0:T(8,128)S(1)} %slice.28, bf16[1,2,48,1536]{3,2,1,0:T(8,128)(2,1)S(1)} %copy-done.1), kind=kOutput, calls=%fused_computation.28 | convolution fusion | flops 1812676608 | bytes 8454144 | tf_op jit(solution)/shard_map/dot_general | solution.py:84
  (41 shorter events, 13.4 us)
Async XLA Ops:
  6.5 54.7 %copy-start = (f32[2,48,1536]{2,1,0:T(8,128)S(1)}, f32[2,48,1536]{2,1,0:T(8,128)}, u32[]{:S(2)}) copy-start(f32[2,48,1536]{2,1,0:T(8,128)} %param.6) | copy-start | bytes 1769476
  6.5 2.3 %copy-start.1 = (bf16[1,2,48,1536]{3,2,1,0:T(8,128)(2,1)S(1)}, bf16[1,2,48,1536]{3,2,1,0:T(8,128)(2,1)}, u32[]{:S(2)}) copy-start(bf16[1,2,48,1536]{3,2,1,0:T(8,128)(2,1)} %param.5) | copy-start | bytes 884740
  6.5 130.4 %reduce-scatter.4.cloned.1.call-start = ((), (), s32[]{:S(2)}) async-start(), calls=%async_computation.4 | async-start | bytes 2506752
  69.5 15.1 %copy-start.2 = (s32[2]{0:T(128)S(1)}, s32[2]{0:T(128)}, u32[]{:S(2)}) copy-start(s32[2]{0:T(128)} %param.7) | copy-start | bytes 28
  72.6 26.0 %all-to-all-start.1 = ((f32[16,1,6144]{2,1,0:T(1,128)}), f32[16,1,6144]{2,1,0:T(1,128)S(1)}, u32[]{:S(2)}, u32[]{:S(2)}) async-start(f32[16,1,6144]{2,1,0:T(1,128)} %reshape.184), calls=%async_computation.1 | async-start | bytes 786432 | tf_op jit(solution)/shard_map/all_to_all | solution.py:71
  128.3 18.8 %all-to-all-start.2 = ((f32[16,1,6144]{2,1,0:T(1,128)}), f32[16,1,6144]{2,1,0:T(1,128)S(1)}, u32[]{:S(2)}, u32[]{:S(2)}) async-start(f32[16,1,6144]{2,1,0:T(1,128)} %reshape.186), calls=%async_computation.2 | async-start | bytes 786432 | tf_op jit(solution)/shard_map/all_to_all | solution.py:82
  148.4 55.4 %all-to-all-start = ((f32[16,2,2,48,96]{4,3,2,1,0:T(8,128)}), f32[16,2,2,48,96]{4,3,2,1,0:T(8,128)S(1)}, u32[]{:S(2)}, u32[]{:S(2)}) async-start(f32[16,2,2,48,96]{4,3,2,1,0:T(8,128)} %broadcast_in_dim.38), calls=%async_computation | async-start | bytes 3145728 | tf_op jit(solution)/shard_map/all_to_all | solution.py:23
Sparse Core Ops, SparseCore 0:
  26.2 99.7 reduce-scatter.3
where the time goes:
time: 224 us; the launch traced here: 220 us
  waiting for transfers between devices  56.4 us (25%)
  local copies, waits for them, and re-layouts  55.3 us (25%)
  matrix products  38.2 us (17%)
  starting transfers between devices  32.1 us (14%)
  other arithmetic  24.1 us (11%)
  between operations  13.9 us (6%)
    all_to_all x1, waiting for transfers between devices, copy_for_each(): lax.all_to_all(jnp.broadcast_to(array[None], (size, *array.shape)), axis,...  35.1 us
    unnamed x17, local copies, waits for them, and re-layouts  26.2 us
    all_to_all x1, waiting for transfers between devices, truncated(): lax.all_to_all(coef, 'band', split_axis=2, concat_axis=1, tiled=True)  13.2 us
    sin x1, other arithmetic, zonal_table(): jnp.sin(phase)  12.9 us
    dot_general x1, matrix products, truncated(): jnp.einsum('ki,lim->lkm', cosines, waves, precision=lax.Precision.HIGHEST)  12 us
    all_to_all x1, starting transfers between devices, truncated(): lax.all_to_all(coef, 'band', split_axis=2, concat_axis=1, tiled=True)  11.9 us
    all_to_all x1, starting transfers between devices, copy_for_each(): lax.all_to_all(jnp.broadcast_to(array[None], (size, *array.shape)), axis,...  11.5 us
    dot_general x1, matrix products, truncated(): jnp.einsum('ki,lkm->lim', cosines, jnp.where(keep, spec, 0.0), precision=...  10.6 us
  transfers between devices with their start and end apart: 4, of which 3 were waited for; matrix products, arithmetic and copies ran while one was open for 40% of the time, Pallas kernels for 0%

commit v1 on v0

v1 whole, which is shorter than its diff:
```python
import functools
import math

import jax
import jax.numpy as jnp
from jax import lax
from jax.experimental import pallas as pl
from jax.experimental.pallas import tpu as pltpu
from jax.sharding import PartitionSpec as P

MESH = pl.DeviceIdType.MESH
F32 = jnp.float32
BF16 = jnp.bfloat16

NX, NZ = 4, 4
BANDS, SIDE = 16, 8
LEV, ROWS, NLON = 2, 48, 1536
NLAT = BANDS * ROWS
KEEP = 512
MEMBERS = NX * NZ
QUARTER = LEV * ROWS // NX
T = 3
R = QUARTER // T
BLOCK = NLON // NZ
GROUPS = 8
WAVES = 64
COLS = 2 * WAVES

RELAX = 0.85
SPREAD_FLOOR = 0.25

COS_TERMS = [(-1.0) ** k / math.factorial(2 * k) for k in range(9)]


def cos_turn(phase, period):
    turns = jnp.floor(phase * (1.0 / period) + 0.5)
    rest = phase - turns * float(period)
    square = rest * rest * ((2.0 * math.pi / period) ** 2)
    total = jnp.full(phase.shape, COS_TERMS[-1], F32)
    for term in COS_TERMS[-2::-1]:
        total = total * square + term
    return total


def halves(values):
    high = values.astype(BF16)
    low = (values - high.astype(F32)).astype(BF16)
    return high, low


def dot(a, b):
    return jnp.dot(a, b, preferred_element_type=F32)


def dot3(a, b):
    return dot(a[0], b[0]) + (dot(a[0], b[1]) + dot(a[1], b[0]))


def iota(shape, dim):
    return lax.broadcasted_iota(jnp.int32, shape, dim)


def inflation(sums):
    count = float(MEMBERS)
    mean_b = sums[0] / count
    mean_a = sums[2] / count
    spread_b = jnp.sqrt(jnp.maximum((sums[1] - count * mean_b * mean_b) / (count - 1), 0.0))
    spread_a = jnp.maximum(
        jnp.sqrt(jnp.maximum((sums[3] - count * mean_a * mean_a) / (count - 1), 0.0)), SPREAD_FLOOR
    )
    factor = 1.0 + RELAX * (spread_b - spread_a) / spread_a
    return factor, mean_b - factor * mean_a


def kernel(
    prior_ref, analysis_ref, inc_ref, trunc_ref, out_ref,
    xs, xr, zs, zr, gr, os, orr, cf, kp, kr,
    f_hi, f_lo, c_hi, c_lo, g_hi, g_lo, sm,
    xs_s, xr_s, zs_s, zr_s, gs_s, gr_s, os_s, or_s, cs_s, cr_s, ks_s, kr_s,
):
    member = lax.axis_index("member")
    band = lax.axis_index("band")
    x, z = member // NZ, lax.rem(member, NZ)
    side, yc = band // SIDE, lax.rem(band, SIDE)
    level = x // 2
    group = lax.rem(x, 2) * NZ + z
    partner = (1 - side) * SIDE + yc

    def at_x(d):
        return lax.rem(x + d, NX)

    def at_z(d):
        return lax.rem(z + d, NZ)

    def at_band(d):
        return side * SIDE + lax.rem(yc + d, SIDE)

    def group_of(d):
        return lax.rem(group + d, GROUPS)

    def group_dev(g):
        return ((level * 2 + g // NZ) * NZ + lax.rem(g, NZ), band)

    def send(src, dst, send_sem, recv_sem, device):
        copy = pltpu.make_async_remote_copy(
            src_ref=src, dst_ref=dst, send_sem=send_sem, recv_sem=recv_sem,
            device_id=device, device_id_type=MESH,
        )
        copy.start()
        sent.append(copy)

    def arrived(dst, recv_sem):
        pltpu.make_async_remote_copy(
            src_ref=dst, dst_ref=dst, send_sem=recv_sem, recv_sem=recv_sem,
            device_id=(member, band), device_id_type=MESH,
        ).wait_recv()

    sent = []

    peers = [(at_x(d) * NZ + z, band) for d in (1, 2, 3)]
    peers += [(x * NZ + at_z(d), band) for d in (1, 2, 3)]
    other = level * 2 + (1 - lax.rem(x, 2))
    peers += [(other * NZ + at_z(d), band) for d in (1, 2, 3)]
    peers += [(member, partner)] + [(member, at_band(d)) for d in range(1, SIDE)]
    barrier = pltpu.get_barrier_semaphore()
    for peer in peers:
        pl.semaphore_signal(barrier, inc=1, device_id=peer, device_id_type=MESH)

    for lev in range(LEV):
        for field, ref in enumerate((prior_ref, analysis_ref)):
            values = ref[0, lev].astype(F32)
            for half in range(2):
                for t in range(T):
                    start = half * QUARTER + t * R
                    xs[lev * 2 + half, t, field] = values[start : start + R]

    pl.semaphore_wait(barrier, len(peers))

    for t in range(T):
        for d in (2, 1, 3):
            q = at_x(d)
            send(xs.at[q, t], xr.at[x, t], xs_s.at[t, q], xr_s.at[t, x], (q * NZ + z, band))

    def zonal_rows(n, _):
        shape = (64, COLS)
        place = (iota(shape, 0) + n * 64).astype(F32)
        lane = iota(shape, 1)
        number = (group * WAVES + lax.rem(lane, WAVES)).astype(F32)
        shifted = jnp.where(lane >= WAVES, float(NLON // 4), 0.0)
        high, low = halves(cos_turn(place * number - shifted, NLON))
        rows = pl.ds(pl.multiple_of(n * 64, 64), 64)
        f_hi[rows, :] = high
        f_lo[rows, :] = low
        return 0

    lax.fori_loop(0, NLON // 64, zonal_rows, 0)
    cf[band] = dot3(halves(inc_ref[level]), (f_hi[...], f_lo[...]))
    for d in range(1, SIDE):
        send(cf.at[band], cf.at[band], cs_s.at[d], cr_s.at[band], (member, at_band(d)))
    send(cf.at[band], cf.at[band], cs_s.at[0], cr_s.at[band], (member, partner))

    def cosine_rows(n, _):
        shape = (16, NLAT)
        order = iota(shape, 0) + n * 16
        place = (2 * iota(shape, 1) + 1).astype(F32)
        scale = jnp.where(order == 0, math.sqrt(1.0 / NLAT), math.sqrt(2.0 / NLAT))
        high, low = halves(scale * cos_turn(order.astype(F32) * place, 4 * NLAT))
        rows = pl.ds(pl.multiple_of(n * 16, 16), 16)
        c_hi[rows, :] = high
        c_lo[rows, :] = low
        return 0

    lax.fori_loop(0, KEEP // 16, cosine_rows, 0)

    arrived(cf.at[partner], cr_s.at[partner])
    for d in range(1, SIDE):
        send(
            cf.at[partner], cf.at[partner], cs_s.at[SIDE + d], cr_s.at[partner],
            (member, at_band(d)),
        )

    def sums_of(t):
        b_sum = b_sq = a_sum = a_sq = None
        for d in range(NX):
            b = xs[x, t, 0] if d == 0 else xr[at_x(d), t, 0]
            a = xs[x, t, 1] if d == 0 else xr[at_x(d), t, 1]
            if d == 0:
                b_sum, b_sq, a_sum, a_sq = b, b * b, a, a * a
            else:
                b_sum, b_sq, a_sum, a_sq = b_sum + b, b_sq + b * b, a_sum + a, a_sq + a * a
        for field, total in enumerate((b_sum, b_sq, a_sum, a_sq)):
            for block in range(NZ):
                zs[t, block, field] = total[:, block * BLOCK : (block + 1) * BLOCK]

    def spread_sums(t):
        for d in (1, 2, 3):
            arrived(xr.at[at_x(d), t], xr_s.at[t, at_x(d)])
        sums_of(t)
        for d in (2, 1, 3):
            to = at_z(d)
            send(zs.at[t, to], zr.at[t, z], zs_s.at[t, to], zr_s.at[t, z], (x * NZ + to, band))

    spread_sums(0)

    for d in range(1, SIDE):
        arrived(cf.at[at_band(d)], cr_s.at[at_band(d)])
        far = (1 - side) * SIDE + lax.rem(yc + d, SIDE)
        arrived(cf.at[far], cr_s.at[far])
    spec = dot3((c_hi[...], c_lo[...]), halves(cf[...].reshape(NLAT, COLS)))
    order = iota((KEEP, COLS), 0)
    number = group * WAVES + lax.rem(iota((KEEP, COLS), 1), WAVES)
    limit = trunc_ref[level]
    spec = jnp.where(order * order + number * number <= limit * limit, spec, 0.0)
    shape = (ROWS, KEEP)
    place = (2 * (iota(shape, 0) + band * ROWS) + 1).astype(F32)
    order = iota(shape, 1)
    scale = jnp.where(order == 0, math.sqrt(1.0 / NLAT), math.sqrt(2.0 / NLAT))
    back = halves(scale * cos_turn(order.astype(F32) * place, 4 * NLAT))
    kept = dot3(back, halves(spec))
    kp[0] = kept[:QUARTER]
    kp[1] = kept[QUARTER:]
    kr[group] = kp[group // NZ]
    for d in range(1, GROUPS):
        g = group_of(d)
        send(kp.at[g // NZ], kr.at[group], ks_s.at[d], kr_s.at[group], group_dev(g))

    spread_sums(1)

    def inverse_rows(n, _):
        shape = (32, BLOCK)
        row = iota(shape, 0) + n * 32
        number = (row // COLS) * WAVES + lax.rem(row, WAVES)
        place = (iota(shape, 1) + z * BLOCK).astype(F32)
        shifted = jnp.where(lax.rem(row, COLS) >= WAVES, float(NLON // 4), 0.0)
        weight = jnp.where(number == 0, 1.0 / NLON, 2.0 / NLON)
        high, low = halves(weight * cos_turn(place * number.astype(F32) - shifted, NLON))
        rows = pl.ds(pl.multiple_of(n * 32, 32), 32)
        g_hi[rows, :] = high
        g_lo[rows, :] = low
        return 0

    lax.fori_loop(0, GROUPS * COLS // 32, inverse_rows, 0)

    for t in range(2, T):
        spread_sums(t)

    for d in range(1, GROUPS):
        arrived(kr.at[group_of(d)], kr_s.at[group_of(d)])
    lines = jnp.concatenate([kr[g] for g in range(GROUPS)], axis=1)
    sm[...] = dot3(halves(lines), (g_hi[...], g_lo[...]))

    for t in range(T):
        for d in (1, 2, 3):
            arrived(zr.at[t, at_z(d)], zr_s.at[t, at_z(d)])
        total = zs[t, z]
        for d in (1, 2, 3):
            total = total + zr[t, at_z(d)]
        factor, shift = inflation([total[field] for field in range(4)])
        gr[t, z, 0] = factor
        gr[t, z, 1] = shift + sm[t * R : (t + 1) * R]
        for d in (2, 1, 3):
            to = at_z(d)
            send(gr.at[t, z], gr.at[t, z], gs_s.at[t, to], gr_s.at[t, z], (x * NZ + to, band))

    for t in range(T):
        for d in (1, 2, 3):
            arrived(gr.at[t, at_z(d)], gr_s.at[t, at_z(d)])
        factor = jnp.concatenate([gr[t, block, 0] for block in range(NZ)], axis=1)
        shift = jnp.concatenate([gr[t, block, 1] for block in range(NZ)], axis=1)
        for d in (2, 1, 3):
            q = at_x(d)
            os[q, t] = shift + factor * xr[q, t, 1]
            send(os.at[q, t], orr.at[x, t], os_s.at[t, q], or_s.at[t, x], (q * NZ + z, band))
        orr[x, t] = shift + factor * xs[x, t, 1]

    for t in range(T):
        for d in (1, 2, 3):
            arrived(orr.at[at_x(d), t], or_s.at[t, at_x(d)])
    for lev in range(LEV):
        out_ref[0, lev] = orr[2 * lev : 2 * lev + 2].reshape(ROWS, NLON).astype(BF16)

    for copy in sent:
        copy.wait_send()


def on_device(prior, analysis, increment, truncation):
    vmem = pl.BlockSpec(memory_space=pltpu.VMEM)
    dma = pltpu.SemaphoreType.DMA
    return pl.pallas_call(
        kernel,
        out_shape=jax.ShapeDtypeStruct((1, LEV, ROWS, NLON), BF16),
        in_specs=[vmem, vmem, vmem, pl.BlockSpec(memory_space=pltpu.SMEM)],
        out_specs=vmem,
        scratch_shapes=[
            pltpu.VMEM((NX, T, 2, R, NLON), F32),
            pltpu.VMEM((NX, T, 2, R, NLON), F32),
            pltpu.VMEM((T, NZ, 4, R, BLOCK), F32),
            pltpu.VMEM((T, NZ, 4, R, BLOCK), F32),
            pltpu.VMEM((T, NZ, 2, R, BLOCK), F32),
            pltpu.VMEM((NX, T, R, NLON), F32),
            pltpu.VMEM((NX, T, R, NLON), F32),
            pltpu.VMEM((BANDS, ROWS, COLS), F32),
            pltpu.VMEM((2, QUARTER, COLS), F32),
            pltpu.VMEM((GROUPS, QUARTER, COLS), F32),
            pltpu.VMEM((NLON, COLS), BF16),
            pltpu.VMEM((NLON, COLS), BF16),
            pltpu.VMEM((KEEP, NLAT), BF16),
            pltpu.VMEM((KEEP, NLAT), BF16),
            pltpu.VMEM((GROUPS * COLS, BLOCK), BF16),
            pltpu.VMEM((GROUPS * COLS, BLOCK), BF16),
            pltpu.VMEM((QUARTER, BLOCK), F32),
            dma((T, NX)), dma((T, NX)),
            dma((T, NZ)), dma((T, NZ)),
            dma((T, NZ)), dma((T, NZ)),
            dma((T, NX)), dma((T, NX)),
            dma((2 * SIDE,)), dma((BANDS,)),
            dma((GROUPS,)), dma((GROUPS,)),
        ],
        compiler_params=pltpu.CompilerParams(collective_id=0, has_side_effects=True),
    )(prior, analysis, increment, truncation)


def solution(mesh):
    placed = (
        P("member", None, "band", None),
        P("member", None, "band", None),
        P(None, "band", None),
        P(),
    )
    return jax.shard_map(
        on_device,
        mesh=mesh,
        in_specs=placed,
        out_specs=P("member", None, "band", None),
        check_vma=False,
    )
```

time: 224 us -> 49.2 us (0.22); the launches traced: 220 us -> 48.6 us
  waiting for transfers between devices: 56.4 us -> 0 us
  local copies, waits for them, and re-layouts: 55.3 us -> 1.69 us
  Pallas kernels: 0 us -> 46.9 us
  matrix products: 38.2 us -> 0 us
  starting transfers between devices: 32.1 us -> 0 us
  other arithmetic: 24.1 us -> 0 us
  between operations: 13.9 us -> 0.01 us
    all_to_all x3 -> x0, waiting for transfers between devices: 56.4 us -> none  [the longest x1 35.1 us: copy_for_each(): lax.all_to_all(jnp.broadcast_to(array[None], (size, *array.shape)), axis,...]
    pallas_call x0 -> x1, Pallas kernels: none -> 46.9 us  [on_device(): pl.pallas_call(kernel, out_shape=jax.ShapeDtypeStruct((1, LEV, ROWS, NLON...]
    dot_general x4 -> x0, matrix products: 38.2 us -> none  [the longest x1 12 us: truncated(): jnp.einsum('ki,lim->lkm', cosines, waves, precision=lax.Precision.HIGHEST)]
    all_to_all x3 -> x0, starting transfers between devices: 32.1 us -> none  [the longest x1 11.9 us: truncated(): lax.all_to_all(coef, 'band', split_axis=2, concat_axis=1, tiled=True)]
    unnamed x17 -> x1, local copies, waits for them, and re-layouts: 26.2 us -> 1.69 us
    sin x1 -> x0, other arithmetic: 12.9 us -> none  [zonal_table(): jnp.sin(phase)]
    another operation x1 -> x0, local copies, waits for them, and re-layouts: 10.4 us -> none  [zonal_table(): jnp.stack([jnp.cos(phase), jnp.sin(phase)], axis=2).reshape(nlon, 2 * waves)]
    reshape x2 -> x0, local copies, waits for them, and re-layouts: 9 us -> none  [the longest x1 8.45 us: zonal_table(): jnp.stack([jnp.cos(phase), jnp.sin(phase)], axis=2).reshape(nlon, 2 * waves)]
  transfers between devices with their start and end apart: 4 -> 0, of which waited for: 3 -> 0; matrix products, arithmetic and copies ran while one was open for 40% -> 0% of each run, Pallas kernels for 0% -> 0%
where the time goes in v1:
time: 49.2 us; the launch traced here: 48.6 us
  Pallas kernels  46.9 us (95%)
  local copies, waits for them, and re-layouts  1.69 us (3%)
    pallas_call x1, Pallas kernels, on_device(): pl.pallas_call(kernel, out_shape=jax.ShapeDtypeStruct((1, LEV, ROWS, NLON...  46.9 us
    unnamed x1, local copies, waits for them, and re-layouts  1.69 us

profile of v1, /device:TPU:8, one launch (start us, length us, event | category | flops | bytes accessed | tf_op | source)
XLA Modules:
  0.0 48.6 jit_solution(16897824500438479569)
XLA Ops:
  0.0 46.9 %shard_map.46 = bf16[1,2,48,1536]{3,2,1,0:T(8,128)(2,1)} custom-call(bf16[1,2,48,1536]{3,2,1,0:T(8,128)(2,1)} %prior_ref.1, bf16[1,2,48,1536]{3,2,1,0:T(8,128)(2,1)} %analysis_ref.1, f32[2,48,1536]{2,1,0:T(8,128)} %inc_ref.1, s32[2]{0:T(128)} %trunc_ref.1), custom_call_target="tpu_custom_call" | custom-call | tf_op jit(solution)/shard_map/pallas_call | solution.py:289
  46.9 1.7 %copy.6 = bf16[1,2,48,1536]{3,2,1,0:T(8,128)(2,1)} copy(bf16[1,2,48,1536]{3,2,1,0:T(8,128)(2,1)} %shard_map.46) | data formatting | bytes 589824

commit v2 on v1

v2 whole, which is shorter than its diff:
```python
import functools
import math

import jax
import jax.numpy as jnp
from jax import lax
from jax.experimental import pallas as pl
from jax.experimental.pallas import tpu as pltpu
from jax.sharding import PartitionSpec as P

MESH = pl.DeviceIdType.MESH
F32 = jnp.float32
BF16 = jnp.bfloat16

NX, NZ = 4, 4
BANDS, SIDE = 16, 8
LEV, ROWS, NLON = 2, 48, 1536
NLAT = BANDS * ROWS
KEEP = 512
MEMBERS = NX * NZ
QUARTER = LEV * ROWS // NX
R = 8
WIDTH = 512
PARTS = NLON // WIDTH
T = QUARTER // R * PARTS
PIECE = WIDTH // NZ
BLOCK = NLON // NZ
GROUPS = 8
WAVES = 64
COLS = 2 * WAVES

RELAX = 0.85
SPREAD_FLOOR = 0.25

COS_TERMS = [(-1.0) ** k / math.factorial(2 * k) for k in range(9)]


def cos_turn(phase, period):
    turns = jnp.floor(phase * (1.0 / period) + 0.5)
    rest = phase - turns * float(period)
    square = rest * rest * ((2.0 * math.pi / period) ** 2)
    total = jnp.full(phase.shape, COS_TERMS[-1], F32)
    for term in COS_TERMS[-2::-1]:
        total = total * square + term
    return total


def halves(values):
    high = values.astype(BF16)
    low = (values - high.astype(F32)).astype(BF16)
    return high, low


def dot(a, b):
    return jnp.dot(a, b, preferred_element_type=F32)


def dot3(a, b):
    return dot(a[0], b[0]) + (dot(a[0], b[1]) + dot(a[1], b[0]))


def iota(shape, dim):
    return lax.broadcasted_iota(jnp.int32, shape, dim)


def inflation(sums):
    count = float(MEMBERS)
    mean_b = sums[0] / count
    mean_a = sums[2] / count
    spread_b = jnp.sqrt(jnp.maximum((sums[1] - count * mean_b * mean_b) / (count - 1), 0.0))
    spread_a = jnp.maximum(
        jnp.sqrt(jnp.maximum((sums[3] - count * mean_a * mean_a) / (count - 1), 0.0)), SPREAD_FLOOR
    )
    factor = 1.0 + RELAX * (spread_b - spread_a) / spread_a
    return factor, mean_b - factor * mean_a


def kernel(
    prior_ref, analysis_ref, inc_ref, trunc_ref, out_ref,
    prior, analysis, inc, trunc, xs, xr, zs, zr, zc, gr, os, cf, kp, kr,
    f_hi, f_lo, c_hi, c_lo, g_hi, g_lo, sm,
    xs_s, xr_s, zs_s, zr_s, gs_s, gr_s, os_s, or_s, cs_s, cr_s, ks_s, kr_s, in_s, reach,
):
    member = lax.axis_index("member")
    band = lax.axis_index("band")
    x, z = member // NZ, lax.rem(member, NZ)
    side, yc = band // SIDE, lax.rem(band, SIDE)
    level = x // 2
    group = lax.rem(x, 2) * NZ + z
    partner = (1 - side) * SIDE + yc
    line = side * NZ + z

    def at_x(d):
        return lax.rem(x + d, NX)

    def at_z(d):
        return lax.rem(z + d, NZ)

    def at_band(d):
        return side * SIDE + lax.rem(yc + d, SIDE)

    def group_of(d):
        return lax.rem(group + d, GROUPS)

    def group_dev(g):
        return ((level * 2 + g // NZ) * NZ + lax.rem(g, NZ), band)

    def on_line(place):
        return (x * NZ + lax.rem(place, NZ), place // NZ * SIDE + yc)

    def send(src, dst, send_sem, recv_sem, device):
        copy = pltpu.make_async_remote_copy(
            src_ref=src, dst_ref=dst, send_sem=send_sem, recv_sem=recv_sem,
            device_id=device, device_id_type=MESH,
        )
        copy.start()
        return copy

    def left(src, send_sem):
        pltpu.make_async_remote_copy(
            src_ref=src, dst_ref=src, send_sem=send_sem, recv_sem=send_sem,
            device_id=(member, band), device_id_type=MESH,
        ).wait_send()

    def arrived(dst, recv_sem):
        pltpu.make_async_remote_copy(
            src_ref=dst, dst_ref=dst, send_sem=recv_sem, recv_sem=recv_sem,
            device_id=(member, band), device_id_type=MESH,
        ).wait_recv()

    loads = [
        pltpu.make_async_copy(prior_ref.at[0], prior, in_s.at[0]),
        pltpu.make_async_copy(analysis_ref.at[0], analysis, in_s.at[1]),
        pltpu.make_async_copy(inc_ref.at[level], inc, in_s.at[2]),
        pltpu.make_async_copy(trunc_ref, trunc, in_s.at[3]),
    ]
    for load in loads:
        load.start()

    peers = [(at_x(d) * NZ + z, band) for d in (1, 2, 3)]
    peers += [(member, at_band(d)) for d in range(1, SIDE)]
    barrier = pltpu.get_barrier_semaphore()

    def tell_line(semaphore):
        @pl.when(line > 0)
        def _():
            pl.semaphore_signal(
                semaphore, inc=1, device_id=on_line(line - 1), device_id_type=MESH
            )

        @pl.when(line < 2 * NZ - 1)
        def _():
            pl.semaphore_signal(
                semaphore, inc=1, device_id=on_line(line + 1), device_id_type=MESH
            )

    beside = (line > 0).astype(jnp.int32) + (line < 2 * NZ - 1).astype(jnp.int32)
    for peer in peers:
        pl.semaphore_signal(barrier, inc=1, device_id=peer, device_id_type=MESH)
    tell_line(barrier)

    def tell(stage):
        tell_line(reach.at[stage])

    def told(stage):
        pl.semaphore_wait(reach.at[stage], beside)

    def zonal_rows(n, _):
        shape = (64, COLS)
        place = (iota(shape, 0) + n * 64).astype(F32)
        lane = iota(shape, 1)
        number = (group * WAVES + lax.rem(lane, WAVES)).astype(F32)
        shifted = jnp.where(lane >= WAVES, float(NLON // 4), 0.0)
        high, low = halves(cos_turn(place * number - shifted, NLON))
        rows = pl.ds(pl.multiple_of(n * 64, 64), 64)
        f_hi[rows, :] = high
        f_lo[rows, :] = low
        return 0

    def cosine_rows(n, _):
        shape = (16, NLAT)
        order = iota(shape, 0) + n * 16
        place = (2 * iota(shape, 1) + 1).astype(F32)
        scale = jnp.where(order == 0, math.sqrt(1.0 / NLAT), math.sqrt(2.0 / NLAT))
        high, low = halves(scale * cos_turn(order.astype(F32) * place, 4 * NLAT))
        rows = pl.ds(pl.multiple_of(n * 16, 16), 16)
        c_hi[rows, :] = high
        c_lo[rows, :] = low
        return 0

    def inverse_rows(n, _):
        shape = (32, BLOCK)
        row = iota(shape, 0) + n * 32
        number = (row // COLS) * WAVES + lax.rem(row, WAVES)
        lane = iota(shape, 1)
        place = (lane // PIECE * WIDTH + z * PIECE + lax.rem(lane, PIECE)).astype(F32)
        shifted = jnp.where(lax.rem(row, COLS) >= WAVES, float(NLON // 4), 0.0)
        weight = jnp.where(number == 0, 1.0 / NLON, 2.0 / NLON)
        high, low = halves(weight * cos_turn(place * number.astype(F32) - shifted, NLON))
        rows = pl.ds(pl.multiple_of(n * 32, 32), 32)
        g_hi[rows, :] = high
        g_lo[rows, :] = low
        return 0

    cosine_steps = KEEP // 16
    inverse_steps = GROUPS * COLS // 32

    end = (z == 0) | (z == NZ - 1)
    middle = jnp.logical_not(end)
    start = jnp.where(z < 2, 1, 0)
    beyond = jnp.where(z < 2, 1 - z, 5 - z)
    across = 3 - z
    far_end = jnp.where(z == 1, 3, 0)
    other_middle = 3 - z

    def spread_sums(t):
        for d in (1, 3, 2):
            arrived(xr.at[at_x(d), t], xr_s.at[t, at_x(d)])
        b_sum = b_sq = a_sum = a_sq = None
        for d in range(NX):
            b = xs[x, t, 0] if d == 0 else xr[at_x(d), t, 0]
            a = xs[x, t, 1] if d == 0 else xr[at_x(d), t, 1]
            if d == 0:
                b_sum, b_sq, a_sum, a_sq = b, b * b, a, a * a
            else:
                b_sum, b_sq, a_sum, a_sq = b_sum + b, b_sq + b * b, a_sum + a, a_sq + a * a
        for field, total in enumerate((b_sum, b_sq, a_sum, a_sq)):
            for block in range(NZ):
                zs[t, block, field] = total[:, block * PIECE : (block + 1) * PIECE]

        @pl.when(end)
        def _():
            send(
                zs.at[t, pl.ds(start, 3)], zr.at[t, pl.ds(0, 3)], zs_s.at[t, 0], zr_s.at[t, 0],
                (x * NZ + beyond, band),
            )

        @pl.when(middle)
        def _():
            send(
                zs.at[t, beyond], zr.at[t, 0], zs_s.at[t, 0], zr_s.at[t, 0],
                (x * NZ + beyond, band),
            )

    def pass_on(t):
        @pl.when(middle)
        def _():
            arrived(zr.at[t, pl.ds(0, 3)], zr_s.at[t, 0])
            for k, to in enumerate((far_end, other_middle)):
                zc[t, k] = zs[t, to] + zr[t, to - start]
                send(
                    zc.at[t, k], zr.at[t, 3], zs_s.at[t, 1 + k], zr_s.at[t, 1],
                    (x * NZ + to, band),
                )

    def spread_factors(t):
        @pl.when(end)
        def _():
            arrived(zr.at[t, 0], zr_s.at[t, 0])

        arrived(zr.at[t, 3], zr_s.at[t, 1])
        total = zs[t, z] + zr[t, jnp.where(z == 2, 2, 0)] + zr[t, 3]
        factor, shift = inflation([total[field] for field in range(4)])
        gr[t, z, 0] = factor
        gr[t, z, 1] = shift + sm[
            t // PARTS * R : t // PARTS * R + R, t % PARTS * PIECE : (t % PARTS + 1) * PIECE
        ]
        for d in (2, 1, 3):
            to = at_z(d)
            send(gr.at[t, z], gr.at[t, z], gs_s.at[t, to], gr_s.at[t, z], (x * NZ + to, band))

    top = lax.rem(x, 2) * QUARTER

    def update(t):
        for d in (1, 2, 3):
            arrived(gr.at[t, at_z(d)], gr_s.at[t, at_z(d)])
        factor = jnp.concatenate([gr[t, block, 0] for block in range(NZ)], axis=1)
        shift = jnp.concatenate([gr[t, block, 1] for block in range(NZ)], axis=1)
        rows = pl.ds(pl.multiple_of(top + t // PARTS * R, R), R)
        lanes = pl.ds(t % PARTS * WIDTH, WIDTH)
        for d in (2, 1, 3):
            q = at_x(d)
            os[q, t] = shift + factor * xr[q, t, 1]
            send(
                os.at[q, t], out_ref.at[0, level, rows, lanes], os_s.at[t, q], or_s.at[t, x],
                (q * NZ + z, band),
            )
        out_ref[0, level, rows, lanes] = shift + factor * xs[x, t, 1]

    lax.fori_loop(0, NLON // 64, zonal_rows, 0)
    loads[0].wait()
    loads[1].wait()
    for lev in range(LEV):
        for field, ref in enumerate((prior, analysis)):
            values = ref[lev].astype(F32)
            for half in range(2):
                for t in range(T):
                    r = half * QUARTER + t // PARTS * R
                    w = t % PARTS * WIDTH
                    xs[lev * 2 + half, t, field] = values[r : r + R, w : w + WIDTH]

    pl.semaphore_wait(barrier, len(peers) + beside)
    tell(0)
    for t in range(T):
        for d in (2, 1, 3):
            q = at_x(d)
            send(xs.at[q, t], xr.at[x, t], xs_s.at[t, q], xr_s.at[t, x], (q * NZ + z, band))

    loads[2].wait()
    loads[3].wait()
    cf[band] = dot3(halves(inc[...]), (f_hi[...], f_lo[...]))
    for d in range(1, SIDE):
        send(cf.at[band], cf.at[band], cs_s.at[d], cr_s.at[band], (member, at_band(d)))
    told(0)
    tell(1)
    lax.fori_loop(0, cosine_steps // 4, cosine_rows, 0)
    told(1)
    tell(2)
    lax.fori_loop(cosine_steps // 4, cosine_steps // 2, cosine_rows, 0)
    told(2)
    send(cf.at[band], cf.at[band], cs_s.at[0], cr_s.at[band], (member, partner))
    spread_sums(0)
    lax.fori_loop(cosine_steps // 2, cosine_steps, cosine_rows, 0)
    spread_sums(1)
    spread_sums(2)
    pass_on(0)
    spread_sums(3)
    pass_on(1)
    arrived(cf.at[partner], cr_s.at[partner])
    for d in range(1, SIDE):
        send(
            cf.at[partner], cf.at[partner], cs_s.at[SIDE + d], cr_s.at[partner],
            (member, at_band(d)),
        )
    lax.fori_loop(0, inverse_steps // 2, inverse_rows, 0)
    spread_sums(4)
    pass_on(2)
    lax.fori_loop(inverse_steps // 2, inverse_steps, inverse_rows, 0)
    spread_sums(5)
    pass_on(3)

    for d in range(1, SIDE):
        arrived(cf.at[at_band(d)], cr_s.at[at_band(d)])
        far = (1 - side) * SIDE + lax.rem(yc + d, SIDE)
        arrived(cf.at[far], cr_s.at[far])
    spec = dot3((c_hi[...], c_lo[...]), halves(cf[...].reshape(NLAT, COLS)))
    order = iota((KEEP, COLS), 0)
    number = group * WAVES + lax.rem(iota((KEEP, COLS), 1), WAVES)
    limit = trunc[level]
    spec = jnp.where(order * order + number * number <= limit * limit, spec, 0.0)
    shape = (ROWS, KEEP)
    place = (2 * (iota(shape, 0) + band * ROWS) + 1).astype(F32)
    order = iota(shape, 1)
    scale = jnp.where(order == 0, math.sqrt(1.0 / NLAT), math.sqrt(2.0 / NLAT))
    back = halves(scale * cos_turn(order.astype(F32) * place, 4 * NLAT))
    kept = dot3(back, halves(spec))
    kp[0] = kept[:QUARTER]
    kp[1] = kept[QUARTER:]
    kr[group] = kp[group // NZ]
    for d in range(1, GROUPS):
        g = group_of(d)
        send(kp.at[g // NZ], kr.at[group], ks_s.at[d], kr_s.at[group], group_dev(g))

    for t in range(6, T):
        spread_sums(t)
        pass_on(t - 2)
    pass_on(T - 2)
    pass_on(T - 1)

    for d in range(1, GROUPS):
        arrived(kr.at[group_of(d)], kr_s.at[group_of(d)])
    lines = jnp.concatenate([kr[g] for g in range(GROUPS)], axis=1)
    sm[...] = dot3(halves(lines), (g_hi[...], g_lo[...]))

    for t in range(T):
        spread_factors(t)
    for t in range(T):
        update(t)

    for t in range(T):
        for d in (1, 2, 3):
            q = at_x(d)
            rows = pl.ds(pl.multiple_of(lax.rem(q, 2) * QUARTER + t // PARTS * R, R), R)
            arrived(
                out_ref.at[0, q // 2, rows, pl.ds(t % PARTS * WIDTH, WIDTH)], or_s.at[t, q]
            )

    for t in range(T):
        for d in (1, 2, 3):
            left(xs.at[at_x(d), t], xs_s.at[t, at_x(d)])
            left(gr.at[t, z], gs_s.at[t, at_z(d)])
            left(os.at[at_x(d), t], os_s.at[t, at_x(d)])
    for d in range(1, SIDE):
        left(cf.at[band], cs_s.at[d])
        left(cf.at[partner], cs_s.at[SIDE + d])
        left(kp.at[group_of(d) // NZ], ks_s.at[d])
    left(cf.at[band], cs_s.at[0])

    @pl.when(end)
    def _():
        for t in range(T):
            left(zs.at[t, pl.ds(start, 3)], zs_s.at[t, 0])

    @pl.when(middle)
    def _():
        for t in range(T):
            left(zs.at[t, beyond], zs_s.at[t, 0])
            left(zc.at[t, 0], zs_s.at[t, 1])
            left(zc.at[t, 1], zs_s.at[t, 2])


def on_device(prior, analysis, increment, truncation):
    vmem = pl.BlockSpec(memory_space=pltpu.VMEM)
    hbm = pl.BlockSpec(memory_space=pltpu.HBM)
    dma = pltpu.SemaphoreType.DMA
    return pl.pallas_call(
        kernel,
        out_shape=pltpu.VMEM((1, LEV, ROWS, NLON), F32),
        in_specs=[hbm, hbm, hbm, hbm],
        out_specs=vmem,
        scratch_shapes=[
            pltpu.VMEM((LEV, ROWS, NLON), BF16),
            pltpu.VMEM((LEV, ROWS, NLON), BF16),
            pltpu.VMEM((ROWS, NLON), F32),
            pltpu.SMEM((LEV,), jnp.int32),
            pltpu.VMEM((NX, T, 2, R, WIDTH), F32),
            pltpu.VMEM((NX, T, 2, R, WIDTH), F32),
            pltpu.VMEM((T, NZ, 4, R, PIECE), F32),
            pltpu.VMEM((T, NZ, 4, R, PIECE), F32),
            pltpu.VMEM((T, 2, 4, R, PIECE), F32),
            pltpu.VMEM((T, NZ, 2, R, PIECE), F32),
            pltpu.VMEM((NX, T, R, WIDTH), F32),
            pltpu.VMEM((BANDS, ROWS, COLS), F32),
            pltpu.VMEM((2, QUARTER, COLS), F32),
            pltpu.VMEM((GROUPS, QUARTER, COLS), F32),
            pltpu.VMEM((NLON, COLS), BF16),
            pltpu.VMEM((NLON, COLS), BF16),
            pltpu.VMEM((KEEP, NLAT), BF16),
            pltpu.VMEM((KEEP, NLAT), BF16),
            pltpu.VMEM((GROUPS * COLS, BLOCK), BF16),
            pltpu.VMEM((GROUPS * COLS, BLOCK), BF16),
            pltpu.VMEM((QUARTER, BLOCK), F32),
            dma((T, NX)), dma((T, NX)),
            dma((T, NZ)), dma((T, NZ)),
            dma((T, NZ)), dma((T, NZ)),
            dma((T, NX)), dma((T, NX)),
            dma((2 * SIDE,)), dma((BANDS,)),
            dma((GROUPS,)), dma((GROUPS,)),
            dma((4,)), pltpu.SemaphoreType.REGULAR((3,)),
        ],
        compiler_params=pltpu.CompilerParams(collective_id=0, has_side_effects=True),
    )(prior, analysis, increment, truncation).astype(BF16)


def solution(mesh):
    placed = (
        P("member", None, "band", None),
        P("member", None, "band", None),
        P(None, "band", None),
        P(),
    )
    return jax.shard_map(
        on_device,
        mesh=mesh,
        in_specs=placed,
        out_specs=P("member", None, "band", None),
        check_vma=False,
    )
```

time: 49.2 us -> 47 us (0.955)
  local copies, waits for them, and re-layouts: 1.69 us -> 0 us
  Pallas kernels: 46.9 us -> 45.7 us
  other arithmetic: 0 us -> 0.75 us
    unnamed x1 -> x0, local copies, waits for them, and re-layouts: 1.69 us -> none
    pallas_call x1, Pallas kernels: 46.9 us -> 45.7 us  [on_device(): pl.pallas_call(kernel, out_shape=pltpu.VMEM((1, LEV, ROWS, NLON), F32), i...]
    convert_element_type x0 -> x1, other arithmetic: none -> 0.75 us  [on_device(): return pl.pallas_call(kernel, out_shape=pltpu.VMEM((1, LEV, ROWS, NLON),...]
where the time goes in v2:
time: 47 us; the launch traced here: 46.4 us
  Pallas kernels  45.7 us (97%)
  other arithmetic  0.75 us (2%)
    pallas_call x1, Pallas kernels, on_device(): pl.pallas_call(kernel, out_shape=pltpu.VMEM((1, LEV, ROWS, NLON), F32), i...  45.7 us

profile of v2, /device:TPU:8, one launch (start us, length us, event | category | flops | bytes accessed | tf_op | source)
XLA Modules:
  0.0 46.4 jit_solution(10992230144675478274)
XLA Ops:
  0.0 45.7 %shard_map.46 = f32[1,2,48,1536]{3,2,1,0:T(8,128)S(1)} custom-call(bf16[1,2,48,1536]{3,2,1,0:T(8,128)(2,1)} %prior_ref.1, bf16[1,2,48,1536]{3,2,1,0:T(8,128)(2,1)} %analysis_ref.1, f32[2,48,1536]{2,1,0:T(8,128)} %inc_ref.1, s32[2]{0:T(128)} %trunc_ref.1), custom_call_target="tpu_custom_call" | custom-call | tf_op jit(solution)/shard_map/pallas_call | solution.py:416
  45.7 0.7 %convert_element_type.3 = bf16[1,2,48,1536]{3,2,1,0:T(8,128)(2,1)} convert(f32[1,2,48,1536]{3,2,1,0:T(8,128)S(1)} %shard_map.46) | non-fusion elementwise | flops 147456 | bytes 884736 | tf_op jit(solution)/shard_map/convert_element_type | solution.py:452

commit v3 on v2

--- a/solution.py
+++ b/solution.py
@@ -77,7 +77,7 @@
 
 def kernel(
     prior_ref, analysis_ref, inc_ref, trunc_ref, out_ref,
-    prior, analysis, inc, trunc, xs, xr, zs, zr, zc, gr, os, cf, kp, kr,
+    prior, analysis, inc, trunc, xs, xr, zs, zr, zc, gr, os, cf, ps, pr, kp, kr,
     f_hi, f_lo, c_hi, c_lo, g_hi, g_lo, sm,
     xs_s, xr_s, zs_s, zr_s, gs_s, gr_s, os_s, or_s, cs_s, cr_s, ks_s, kr_s, in_s, reach,
 ):
@@ -88,7 +88,7 @@
     level = x // 2
     group = lax.rem(x, 2) * NZ + z
     partner = (1 - side) * SIDE + yc
-    line = side * NZ + z
+    mate = (level * 2 + 1 - lax.rem(x, 2)) * NZ + z
 
     def at_x(d):
         return lax.rem(x + d, NX)
@@ -104,9 +104,6 @@
 
     def group_dev(g):
         return ((level * 2 + g // NZ) * NZ + lax.rem(g, NZ), band)
-
-    def on_line(place):
-        return (x * NZ + lax.rem(place, NZ), place // NZ * SIDE + yc)
 
     def send(src, dst, send_sem, recv_sem, device):
         copy = pltpu.make_async_remote_copy(
@@ -141,29 +138,25 @@
     peers += [(member, at_band(d)) for d in range(1, SIDE)]
     barrier = pltpu.get_barrier_semaphore()
 
-    def tell_line(semaphore):
-        @pl.when(line > 0)
-        def _():
-            pl.semaphore_signal(
-                semaphore, inc=1, device_id=on_line(line - 1), device_id_type=MESH
-            )
-
-        @pl.when(line < 2 * NZ - 1)
-        def _():
-            pl.semaphore_signal(
-                semaphore, inc=1, device_id=on_line(line + 1), device_id_type=MESH
-            )
-
-    beside = (line > 0).astype(jnp.int32) + (line < 2 * NZ - 1).astype(jnp.int32)
+    near = ((z > 0, member - 1), (z < NZ - 1, member + 1))
+    neighbours = (z > 0).astype(jnp.int32) + (z < NZ - 1).astype(jnp.int32)
+
+    def tell(semaphore):
+        for there, device in near:
+
+            @pl.when(there)
+            def _():
+                pl.semaphore_signal(
+                    semaphore, inc=1, device_id=(device, band), device_id_type=MESH
+                )
+
     for peer in peers:
         pl.semaphore_signal(barrier, inc=1, device_id=peer, device_id_type=MESH)
-    tell_line(barrier)
-
-    def tell(stage):
-        tell_line(reach.at[stage])
-
-    def told(stage):
-        pl.semaphore_wait(reach.at[stage], beside)
+    tell(barrier)
+
+    @pl.when(side == 0)
+    def _():
+        pl.semaphore_signal(barrier, inc=1, device_id=(member, partner), device_id_type=MESH)
 
     def zonal_rows(n, _):
         shape = (64, COLS)
@@ -178,9 +171,9 @@
         return 0
 
     def cosine_rows(n, _):
-        shape = (16, NLAT)
+        shape = (16, SIDE * ROWS)
         order = iota(shape, 0) + n * 16
-        place = (2 * iota(shape, 1) + 1).astype(F32)
+        place = (2 * (iota(shape, 1) + side * SIDE * ROWS) + 1).astype(F32)
         scale = jnp.where(order == 0, math.sqrt(1.0 / NLAT), math.sqrt(2.0 / NLAT))
         high, low = halves(scale * cos_turn(order.astype(F32) * place, 4 * NLAT))
         rows = pl.ds(pl.multiple_of(n * 16, 16), 16)
@@ -299,82 +292,92 @@
                     w = t % PARTS * WIDTH
                     xs[lev * 2 + half, t, field] = values[r : r + R, w : w + WIDTH]
 
-    pl.semaphore_wait(barrier, len(peers) + beside)
-    tell(0)
+    pl.semaphore_wait(barrier, len(peers) + neighbours + side)
     for t in range(T):
         for d in (2, 1, 3):
             q = at_x(d)
             send(xs.at[q, t], xr.at[x, t], xs_s.at[t, q], xr_s.at[t, x], (q * NZ + z, band))
+    tell(reach.at[0])
+
+    @pl.when(side == 1)
+    def _():
+        pl.semaphore_signal(reach.at[3], inc=1, device_id=(member, partner), device_id_type=MESH)
+
 
     loads[2].wait()
     loads[3].wait()
-    cf[band] = dot3(halves(inc[...]), (f_hi[...], f_lo[...]))
+    cf[yc] = dot3(halves(inc[...]), (f_hi[...], f_lo[...]))
     for d in range(1, SIDE):
-        send(cf.at[band], cf.at[band], cs_s.at[d], cr_s.at[band], (member, at_band(d)))
-    told(0)
-    tell(1)
-    lax.fori_loop(0, cosine_steps // 4, cosine_rows, 0)
-    told(1)
-    tell(2)
-    lax.fori_loop(cosine_steps // 4, cosine_steps // 2, cosine_rows, 0)
-    told(2)
-    send(cf.at[band], cf.at[band], cs_s.at[0], cr_s.at[band], (member, partner))
+        send(cf.at[yc], cf.at[yc], cs_s.at[d], cr_s.at[yc], (member, at_band(d)))
+    lax.fori_loop(0, cosine_steps, cosine_rows, 0)
+    lax.fori_loop(0, inverse_steps // 2, inverse_rows, 0)
+    pl.semaphore_wait(reach.at[0], neighbours)
+    tell(reach.at[1])
+    lax.fori_loop(inverse_steps // 2, inverse_steps, inverse_rows, 0)
+
+    for d in range(1, SIDE):
+        other = lax.rem(yc + d, SIDE)
+        arrived(cf.at[other], cr_s.at[other])
+    spec = dot3((c_hi[...], c_lo[...]), halves(cf[...].reshape(SIDE * ROWS, COLS)))
+    order = iota((KEEP, COLS), 0)
+    number = group * WAVES + lax.rem(iota((KEEP, COLS), 1), WAVES)
+    limit = trunc[level]
+    spec = jnp.where(order * order + number * number <= limit * limit, spec, 0.0)
+    shape = (2 * ROWS, KEEP)
+    row = iota(shape, 0)
+    place = row + jnp.where(row < ROWS, band, partner - 1) * ROWS
+    order = iota(shape, 1)
+    scale = jnp.where(order == 0, math.sqrt(1.0 / NLAT), math.sqrt(2.0 / NLAT))
+    back = scale * cos_turn(order.astype(F32) * (2 * place + 1).astype(F32), 4 * NLAT)
+    parts = dot3(halves(back), halves(spec))
+    ps[0] = parts[:ROWS]
+    ps[1] = parts[ROWS:]
+
+    @pl.when(side == 0)
+    def _():
+        pl.semaphore_wait(reach.at[3], 1)
+
+    send(ps.at[1], pr, cs_s.at[0], cr_s.at[SIDE], (member, partner))
     spread_sums(0)
-    lax.fori_loop(cosine_steps // 2, cosine_steps, cosine_rows, 0)
+    pl.semaphore_wait(reach.at[1], neighbours)
+    pl.semaphore_signal(reach.at[2], inc=1, device_id=(mate, band), device_id_type=MESH)
     spread_sums(1)
     spread_sums(2)
     pass_on(0)
     spread_sums(3)
     pass_on(1)
-    arrived(cf.at[partner], cr_s.at[partner])
-    for d in range(1, SIDE):
-        send(
-            cf.at[partner], cf.at[partner], cs_s.at[SIDE + d], cr_s.at[partner],
-            (member, at_band(d)),
-        )
-    lax.fori_loop(0, inverse_steps // 2, inverse_rows, 0)
     spread_sums(4)
     pass_on(2)
-    lax.fori_loop(inverse_steps // 2, inverse_steps, inverse_rows, 0)
-    spread_sums(5)
-    pass_on(3)
-
-    for d in range(1, SIDE):
-        arrived(cf.at[at_band(d)], cr_s.at[at_band(d)])
-        far = (1 - side) * SIDE + lax.rem(yc + d, SIDE)
-        arrived(cf.at[far], cr_s.at[far])
-    spec = dot3((c_hi[...], c_lo[...]), halves(cf[...].reshape(NLAT, COLS)))
-    order = iota((KEEP, COLS), 0)
-    number = group * WAVES + lax.rem(iota((KEEP, COLS), 1), WAVES)
-    limit = trunc[level]
-    spec = jnp.where(order * order + number * number <= limit * limit, spec, 0.0)
-    shape = (ROWS, KEEP)
-    place = (2 * (iota(shape, 0) + band * ROWS) + 1).astype(F32)
-    order = iota(shape, 1)
-    scale = jnp.where(order == 0, math.sqrt(1.0 / NLAT), math.sqrt(2.0 / NLAT))
-    back = halves(scale * cos_turn(order.astype(F32) * place, 4 * NLAT))
-    kept = dot3(back, halves(spec))
-    kp[0] = kept[:QUARTER]
-    kp[1] = kept[QUARTER:]
+    pl.semaphore_wait(reach.at[2], 1)
+    arrived(pr, cr_s.at[SIDE])
+    for half in range(2):
+        kp[half] = ps[0, half * QUARTER : (half + 1) * QUARTER] + pr[half * QUARTER : (half + 1) * QUARTER]
     kr[group] = kp[group // NZ]
     for d in range(1, GROUPS):
         g = group_of(d)
         send(kp.at[g // NZ], kr.at[group], ks_s.at[d], kr_s.at[group], group_dev(g))
-
-    for t in range(6, T):
+    for t in range(5, T):
         spread_sums(t)
         pass_on(t - 2)
-    pass_on(T - 2)
-    pass_on(T - 1)
 
     for d in range(1, GROUPS):
         arrived(kr.at[group_of(d)], kr_s.at[group_of(d)])
     lines = jnp.concatenate([kr[g] for g in range(GROUPS)], axis=1)
     sm[...] = dot3(halves(lines), (g_hi[...], g_lo[...]))
 
-    for t in range(T):
+    for t in range(4):
         spread_factors(t)
-    for t in range(T):
+    pass_on(7)
+    spread_factors(4)
+    spread_factors(5)
+    pass_on(8)
+    spread_factors(6)
+    update(0)
+    spread_factors(7)
+    update(1)
+    update(2)
+    spread_factors(8)
+    for t in range(3, T):
         update(t)
 
     for t in range(T):
@@ -391,10 +394,9 @@
             left(gr.at[t, z], gs_s.at[t, at_z(d)])
             left(os.at[at_x(d), t], os_s.at[t, at_x(d)])
     for d in range(1, SIDE):
-        left(cf.at[band], cs_s.at[d])
-        left(cf.at[partner], cs_s.at[SIDE + d])
+        left(cf.at[yc], cs_s.at[d])
         left(kp.at[group_of(d) // NZ], ks_s.at[d])
-    left(cf.at[band], cs_s.at[0])
+    left(ps.at[1], cs_s.at[0])
 
     @pl.when(end)
     def _():
@@ -430,13 +432,15 @@
             pltpu.VMEM((T, 2, 4, R, PIECE), F32),
             pltpu.VMEM((T, NZ, 2, R, PIECE), F32),
             pltpu.VMEM((NX, T, R, WIDTH), F32),
-            pltpu.VMEM((BANDS, ROWS, COLS), F32),
+            pltpu.VMEM((SIDE, ROWS, COLS), F32),
+            pltpu.VMEM((2, ROWS, COLS), F32),
+            pltpu.VMEM((ROWS, COLS), F32),
             pltpu.VMEM((2, QUARTER, COLS), F32),
             pltpu.VMEM((GROUPS, QUARTER, COLS), F32),
             pltpu.VMEM((NLON, COLS), BF16),
             pltpu.VMEM((NLON, COLS), BF16),
-            pltpu.VMEM((KEEP, NLAT), BF16),
-            pltpu.VMEM((KEEP, NLAT), BF16),
+            pltpu.VMEM((KEEP, SIDE * ROWS), BF16),
+            pltpu.VMEM((KEEP, SIDE * ROWS), BF16),
             pltpu.VMEM((GROUPS * COLS, BLOCK), BF16),
             pltpu.VMEM((GROUPS * COLS, BLOCK), BF16),
             pltpu.VMEM((QUARTER, BLOCK), F32),
@@ -444,9 +448,9 @@
             dma((T, NZ)), dma((T, NZ)),
             dma((T, NZ)), dma((T, NZ)),
             dma((T, NX)), dma((T, NX)),
-            dma((2 * SIDE,)), dma((BANDS,)),
+            dma((SIDE,)), dma((SIDE + 1,)),
             dma((GROUPS,)), dma((GROUPS,)),
-            dma((4,)), pltpu.SemaphoreType.REGULAR((3,)),
+            dma((4,)), pltpu.SemaphoreType.REGULAR((4,)),
         ],
         compiler_params=pltpu.CompilerParams(collective_id=0, has_side_effects=True),
     )(prior, analysis, increment, truncation).astype(BF16)

time: 47 us -> 43.7 us (0.930)
  Pallas kernels: 45.7 us -> 42.2 us
    pallas_call x1, Pallas kernels: 45.7 us -> 42.2 us  [on_device(): pl.pallas_call(kernel, out_shape=pltpu.VMEM((1, LEV, ROWS, NLON), F32), i...]
where the time goes in v3:
time: 43.7 us; the launch traced here: 42.9 us
  Pallas kernels  42.2 us (97%)
  other arithmetic  0.75 us (2%)
    pallas_call x1, Pallas kernels, on_device(): pl.pallas_call(kernel, out_shape=pltpu.VMEM((1, LEV, ROWS, NLON), F32), i...  42.2 us

profile of v3, /device:TPU:8, one launch (start us, length us, event | category | flops | bytes accessed | tf_op | source)
XLA Modules:
  0.0 42.9 jit_solution(16928532184735362822)
XLA Ops:
  0.0 42.2 %shard_map.46 = f32[1,2,48,1536]{3,2,1,0:T(8,128)S(1)} custom-call(bf16[1,2,48,1536]{3,2,1,0:T(8,128)(2,1)} %prior_ref.1, bf16[1,2,48,1536]{3,2,1,0:T(8,128)(2,1)} %analysis_ref.1, f32[2,48,1536]{2,1,0:T(8,128)} %inc_ref.1, s32[2]{0:T(128)} %trunc_ref.1), custom_call_target="tpu_custom_call" | custom-call | tf_op jit(solution)/shard_map/pallas_call | solution.py:418
  42.2 0.7 %convert_element_type.3 = bf16[1,2,48,1536]{3,2,1,0:T(8,128)(2,1)} convert(f32[1,2,48,1536]{3,2,1,0:T(8,128)S(1)} %shard_map.46) | non-fusion elementwise | flops 147456 | bytes 884736 | tf_op jit(solution)/shard_map/convert_element_type | solution.py:456

commit v4 on v3

--- a/solution.py
+++ b/solution.py
@@ -20,11 +20,13 @@
 MEMBERS = NX * NZ
 QUARTER = LEV * ROWS // NX
 R = 8
+AT = 6
+EARLY = 5
 WIDTH = 512
 PARTS = NLON // WIDTH
 T = QUARTER // R * PARTS
 PIECE = WIDTH // NZ
-BLOCK = NLON // NZ
+HALF = NLON // 2
 GROUPS = 8
 WAVES = 64
 COLS = 2 * WAVES
@@ -158,11 +160,14 @@
     def _():
         pl.semaphore_signal(barrier, inc=1, device_id=(member, partner), device_id_type=MESH)
 
+    def wave(g, place):
+        return g // 2 * (2 * WAVES) + 2 * place + lax.rem(g, 2)
+
     def zonal_rows(n, _):
         shape = (64, COLS)
         place = (iota(shape, 0) + n * 64).astype(F32)
         lane = iota(shape, 1)
-        number = (group * WAVES + lax.rem(lane, WAVES)).astype(F32)
+        number = wave(group, lax.rem(lane, WAVES)).astype(F32)
         shifted = jnp.where(lane >= WAVES, float(NLON // 4), 0.0)
         high, low = halves(cos_turn(place * number - shifted, NLON))
         rows = pl.ds(pl.multiple_of(n * 64, 64), 64)
@@ -182,21 +187,22 @@
         return 0
 
     def inverse_rows(n, _):
-        shape = (32, BLOCK)
-        row = iota(shape, 0) + n * 32
-        number = (row // COLS) * WAVES + lax.rem(row, WAVES)
-        lane = iota(shape, 1)
-        place = (lane // PIECE * WIDTH + z * PIECE + lax.rem(lane, PIECE)).astype(F32)
+        shape = (16, HALF)
+        row = iota(shape, 0) + n * 16
+        block = n * 16 // COLS
+        g = 2 * lax.rem(block, GROUPS // 2) + block // (GROUPS // 2)
+        number = wave(g, lax.rem(row, WAVES))
         shifted = jnp.where(lax.rem(row, COLS) >= WAVES, float(NLON // 4), 0.0)
         weight = jnp.where(number == 0, 1.0 / NLON, 2.0 / NLON)
+        place = iota(shape, 1).astype(F32)
         high, low = halves(weight * cos_turn(place * number.astype(F32) - shifted, NLON))
-        rows = pl.ds(pl.multiple_of(n * 32, 32), 32)
+        rows = pl.ds(pl.multiple_of(n * 16, 16), 16)
         g_hi[rows, :] = high
         g_lo[rows, :] = low
         return 0
 
     cosine_steps = KEEP // 16
-    inverse_steps = GROUPS * COLS // 32
+    inverse_steps = GROUPS * COLS // 16
 
     end = (z == 0) | (z == NZ - 1)
     middle = jnp.logical_not(end)
@@ -255,12 +261,19 @@
         total = zs[t, z] + zr[t, jnp.where(z == 2, 2, 0)] + zr[t, 3]
         factor, shift = inflation([total[field] for field in range(4)])
         gr[t, z, 0] = factor
-        gr[t, z, 1] = shift + sm[
-            t // PARTS * R : t // PARTS * R + R, t % PARTS * PIECE : (t % PARTS + 1) * PIECE
-        ]
+        gr[t, z, 1] = shift
         for d in (2, 1, 3):
             to = at_z(d)
             send(gr.at[t, z], gr.at[t, z], gs_s.at[t, to], gr_s.at[t, z], (x * NZ + to, band))
+
+    def swap():
+        arrived(pr, cr_s.at[SIDE])
+        for half in range(2):
+            kp[half] = ps[0, half * QUARTER : (half + 1) * QUARTER] + pr[half * QUARTER : (half + 1) * QUARTER]
+        kr[group] = kp[group // NZ]
+        for d in range(1, GROUPS):
+            g = group_of(d)
+            send(kp.at[g // NZ], kr.at[group], ks_s.at[d], kr_s.at[group], group_dev(g))
 
     top = lax.rem(x, 2) * QUARTER
 
@@ -269,6 +282,8 @@
             arrived(gr.at[t, at_z(d)], gr_s.at[t, at_z(d)])
         factor = jnp.concatenate([gr[t, block, 0] for block in range(NZ)], axis=1)
         shift = jnp.concatenate([gr[t, block, 1] for block in range(NZ)], axis=1)
+        row, lane = t // PARTS * R, t % PARTS * WIDTH
+        shift = shift + sm[row : row + R, lane : lane + WIDTH]
         rows = pl.ds(pl.multiple_of(top + t // PARTS * R, R), R)
         lanes = pl.ds(t % PARTS * WIDTH, WIDTH)
         for d in (2, 1, 3):
@@ -292,7 +307,13 @@
                     w = t % PARTS * WIDTH
                     xs[lev * 2 + half, t, field] = values[r : r + R, w : w + WIDTH]
 
+    loads[2].wait()
+    loads[3].wait()
+    cf[yc] = dot3(halves(inc[...]), (f_hi[...], f_lo[...]))
+
     pl.semaphore_wait(barrier, len(peers) + neighbours + side)
+    for d in (4, 5, 3, 2, 6, 7, 1):
+        send(cf.at[yc], cf.at[yc], cs_s.at[d], cr_s.at[yc], (member, at_band(d)))
     for t in range(T):
         for d in (2, 1, 3):
             q = at_x(d)
@@ -304,23 +325,18 @@
         pl.semaphore_signal(reach.at[3], inc=1, device_id=(member, partner), device_id_type=MESH)
 
 
-    loads[2].wait()
-    loads[3].wait()
-    cf[yc] = dot3(halves(inc[...]), (f_hi[...], f_lo[...]))
-    for d in range(1, SIDE):
-        send(cf.at[yc], cf.at[yc], cs_s.at[d], cr_s.at[yc], (member, at_band(d)))
     lax.fori_loop(0, cosine_steps, cosine_rows, 0)
-    lax.fori_loop(0, inverse_steps // 2, inverse_rows, 0)
+    lax.fori_loop(0, 24, inverse_rows, 0)
     pl.semaphore_wait(reach.at[0], neighbours)
     tell(reach.at[1])
-    lax.fori_loop(inverse_steps // 2, inverse_steps, inverse_rows, 0)
+    lax.fori_loop(24, 40, inverse_rows, 0)
 
     for d in range(1, SIDE):
         other = lax.rem(yc + d, SIDE)
         arrived(cf.at[other], cr_s.at[other])
     spec = dot3((c_hi[...], c_lo[...]), halves(cf[...].reshape(SIDE * ROWS, COLS)))
     order = iota((KEEP, COLS), 0)
-    number = group * WAVES + lax.rem(iota((KEEP, COLS), 1), WAVES)
+    number = wave(group, lax.rem(iota((KEEP, COLS), 1), WAVES))
     limit = trunc[level]
     spec = jnp.where(order * order + number * number <= limit * limit, spec, 0.0)
     shape = (2 * ROWS, KEEP)
@@ -341,43 +357,42 @@
     spread_sums(0)
     pl.semaphore_wait(reach.at[1], neighbours)
     pl.semaphore_signal(reach.at[2], inc=1, device_id=(mate, band), device_id_type=MESH)
+    lax.fori_loop(40, 52, inverse_rows, 0)
     spread_sums(1)
+    lax.fori_loop(52, inverse_steps, inverse_rows, 0)
     spread_sums(2)
     pass_on(0)
     spread_sums(3)
     pass_on(1)
-    spread_sums(4)
-    pass_on(2)
     pl.semaphore_wait(reach.at[2], 1)
-    arrived(pr, cr_s.at[SIDE])
-    for half in range(2):
-        kp[half] = ps[0, half * QUARTER : (half + 1) * QUARTER] + pr[half * QUARTER : (half + 1) * QUARTER]
-    kr[group] = kp[group // NZ]
-    for d in range(1, GROUPS):
-        g = group_of(d)
-        send(kp.at[g // NZ], kr.at[group], ks_s.at[d], kr_s.at[group], group_dev(g))
-    for t in range(5, T):
+    for t in range(4, T):
         spread_sums(t)
         pass_on(t - 2)
+        if t == AT:
+            swap()
+        if t == T - 1:
+            spread_factors(0)
+            spread_factors(1)
+    pass_on(T - 2)
+    spread_factors(2)
+    pass_on(T - 1)
+    for t in range(3, EARLY):
+        spread_factors(t)
 
     for d in range(1, GROUPS):
         arrived(kr.at[group_of(d)], kr_s.at[group_of(d)])
-    lines = jnp.concatenate([kr[g] for g in range(GROUPS)], axis=1)
-    sm[...] = dot3(halves(lines), (g_hi[...], g_lo[...]))
-
-    for t in range(4):
+    even = jnp.concatenate([kr[g] for g in range(0, GROUPS, 2)], axis=1)
+    odd = jnp.concatenate([kr[g] for g in range(1, GROUPS, 2)], axis=1)
+    depth = GROUPS * COLS // 2
+    even = dot3(halves(even), (g_hi[:depth], g_lo[:depth]))
+    odd = dot3(halves(odd), (g_hi[depth:], g_lo[depth:]))
+    sm[:, :HALF] = even + odd
+    sm[:, HALF:] = even - odd
+
+    for t in range(EARLY, T):
         spread_factors(t)
-    pass_on(7)
-    spread_factors(4)
-    spread_factors(5)
-    pass_on(8)
-    spread_factors(6)
-    update(0)
-    spread_factors(7)
-    update(1)
-    update(2)
-    spread_factors(8)
-    for t in range(3, T):
+        update(t - EARLY)
+    for t in range(T - EARLY, T):
         update(t)
 
     for t in range(T):
@@ -441,9 +456,9 @@
             pltpu.VMEM((NLON, COLS), BF16),
             pltpu.VMEM((KEEP, SIDE * ROWS), BF16),
             pltpu.VMEM((KEEP, SIDE * ROWS), BF16),
-            pltpu.VMEM((GROUPS * COLS, BLOCK), BF16),
-            pltpu.VMEM((GROUPS * COLS, BLOCK), BF16),
-            pltpu.VMEM((QUARTER, BLOCK), F32),
+            pltpu.VMEM((GROUPS * COLS, HALF), BF16),
+            pltpu.VMEM((GROUPS * COLS, HALF), BF16),
+            pltpu.VMEM((QUARTER, NLON), F32),
             dma((T, NX)), dma((T, NX)),
             dma((T, NZ)), dma((T, NZ)),
             dma((T, NZ)), dma((T, NZ)),

time: 43.7 us -> 42.4 us (0.970); the launches traced: 42.9 us -> 42.3 us
  Pallas kernels: 42.2 us -> 41.6 us
    pallas_call x1, Pallas kernels: 42.2 us -> 41.6 us  [on_device(): pl.pallas_call(kernel, out_shape=pltpu.VMEM((1, LEV, ROWS, NLON), F32), i...]
where the time goes in v4:
time: 42.4 us; the launch traced here: 42.3 us
  Pallas kernels  41.6 us (98%)
  other arithmetic  0.75 us (2%)
    pallas_call x1, Pallas kernels, on_device(): pl.pallas_call(kernel, out_shape=pltpu.VMEM((1, LEV, ROWS, NLON), F32), i...  41.6 us

profile of v4, /device:TPU:8, one launch (start us, length us, event | category | flops | bytes accessed | tf_op | source)
XLA Modules:
  0.0 42.3 jit_solution(655663493195714472)
XLA Ops:
  0.0 41.6 %shard_map.46 = f32[1,2,48,1536]{3,2,1,0:T(8,128)S(1)} custom-call(bf16[1,2,48,1536]{3,2,1,0:T(8,128)(2,1)} %prior_ref.1, bf16[1,2,48,1536]{3,2,1,0:T(8,128)(2,1)} %analysis_ref.1, f32[2,48,1536]{2,1,0:T(8,128)} %inc_ref.1, s32[2]{0:T(128)} %trunc_ref.1), custom_call_target="tpu_custom_call" | custom-call | tf_op jit(solution)/shard_map/pallas_call | solution.py:433
  41.6 0.7 %convert_element_type.3 = bf16[1,2,48,1536]{3,2,1,0:T(8,128)(2,1)} convert(f32[1,2,48,1536]{3,2,1,0:T(8,128)S(1)} %shard_map.46) | non-fusion elementwise | flops 147456 | bytes 884736 | tf_op jit(solution)/shard_map/convert_element_type | solution.py:471

commit v5 on v4

--- a/solution.py
+++ b/solution.py
@@ -20,6 +20,7 @@
 MEMBERS = NX * NZ
 QUARTER = LEV * ROWS // NX
 R = 8
+DIRECT = 6
 AT = 6
 EARLY = 5
 WIDTH = 512
@@ -227,10 +228,21 @@
             for block in range(NZ):
                 zs[t, block, field] = total[:, block * PIECE : (block + 1) * PIECE]
 
+        if t < DIRECT:
+            for d in (2, 1, 3):
+                to = at_z(d)
+                send(zs.at[t, to], zr.at[t, z], zs_s.at[t, d], zr_s.at[t, z], (x * NZ + to, band))
+            return
+
         @pl.when(end)
         def _():
+            far = jnp.where(z == 0, 2, 0)
             send(
-                zs.at[t, pl.ds(start, 3)], zr.at[t, pl.ds(0, 3)], zs_s.at[t, 0], zr_s.at[t, 0],
+                zs.at[t, pl.ds(far, 2)], zr.at[t, pl.ds(far - start, 2)], zs_s.at[t, 0],
+                zr_s.at[t, 0], (x * NZ + beyond, band),
+            )
+            send(
+                zs.at[t, beyond], zr.at[t, beyond - start], zs_s.at[t, 1], zr_s.at[t, 2],
                 (x * NZ + beyond, band),
             )
 
@@ -242,9 +254,12 @@
             )
 
     def pass_on(t):
+        if t < DIRECT:
+            return
+
         @pl.when(middle)
         def _():
-            arrived(zr.at[t, pl.ds(0, 3)], zr_s.at[t, 0])
+            arrived(zr.at[t, pl.ds(jnp.where(z == 1, 1, 0), 2)], zr_s.at[t, 0])
             for k, to in enumerate((far_end, other_middle)):
                 zc[t, k] = zs[t, to] + zr[t, to - start]
                 send(
@@ -253,12 +268,22 @@
                 )
 
     def spread_factors(t):
-        @pl.when(end)
-        def _():
-            arrived(zr.at[t, 0], zr_s.at[t, 0])
-
-        arrived(zr.at[t, 3], zr_s.at[t, 1])
-        total = zs[t, z] + zr[t, jnp.where(z == 2, 2, 0)] + zr[t, 3]
+        if t < DIRECT:
+            total = zs[t, z]
+            for d in (1, 3, 2):
+                arrived(zr.at[t, at_z(d)], zr_s.at[t, at_z(d)])
+                total = total + zr[t, at_z(d)]
+        else:
+            @pl.when(end)
+            def _():
+                arrived(zr.at[t, 0], zr_s.at[t, 0])
+
+            @pl.when(middle)
+            def _():
+                arrived(zr.at[t, jnp.where(z == 2, 2, 0)], zr_s.at[t, 2])
+
+            arrived(zr.at[t, 3], zr_s.at[t, 1])
+            total = zs[t, z] + zr[t, jnp.where(z == 2, 2, 0)] + zr[t, 3]
         factor, shift = inflation([total[field] for field in range(4)])
         gr[t, z, 0] = factor
         gr[t, z, 1] = shift
@@ -335,6 +360,8 @@
         other = lax.rem(yc + d, SIDE)
         arrived(cf.at[other], cr_s.at[other])
     spec = dot3((c_hi[...], c_lo[...]), halves(cf[...].reshape(SIDE * ROWS, COLS)))
+    pl.semaphore_wait(reach.at[1], neighbours)
+    spread_sums(0)
     order = iota((KEEP, COLS), 0)
     number = wave(group, lax.rem(iota((KEEP, COLS), 1), WAVES))
     limit = trunc[level]
@@ -354,16 +381,15 @@
         pl.semaphore_wait(reach.at[3], 1)
 
     send(ps.at[1], pr, cs_s.at[0], cr_s.at[SIDE], (member, partner))
-    spread_sums(0)
-    pl.semaphore_wait(reach.at[1], neighbours)
     pl.semaphore_signal(reach.at[2], inc=1, device_id=(mate, band), device_id_type=MESH)
-    lax.fori_loop(40, 52, inverse_rows, 0)
     spread_sums(1)
-    lax.fori_loop(52, inverse_steps, inverse_rows, 0)
+    lax.fori_loop(40, 48, inverse_rows, 0)
     spread_sums(2)
     pass_on(0)
+    lax.fori_loop(48, 56, inverse_rows, 0)
     spread_sums(3)
     pass_on(1)
+    lax.fori_loop(56, inverse_steps, inverse_rows, 0)
     pl.semaphore_wait(reach.at[2], 1)
     for t in range(4, T):
         spread_sums(t)
@@ -413,14 +439,19 @@
         left(kp.at[group_of(d) // NZ], ks_s.at[d])
     left(ps.at[1], cs_s.at[0])
 
+    for t in range(DIRECT):
+        for d in (1, 2, 3):
+            left(zs.at[t, at_z(d)], zs_s.at[t, d])
+
     @pl.when(end)
     def _():
-        for t in range(T):
-            left(zs.at[t, pl.ds(start, 3)], zs_s.at[t, 0])
+        for t in range(DIRECT, T):
+            left(zs.at[t, pl.ds(jnp.where(z == 0, 2, 0), 2)], zs_s.at[t, 0])
+            left(zs.at[t, beyond], zs_s.at[t, 1])
 
     @pl.when(middle)
     def _():
-        for t in range(T):
+        for t in range(DIRECT, T):
             left(zs.at[t, beyond], zs_s.at[t, 0])
             left(zc.at[t, 0], zs_s.at[t, 1])
             left(zc.at[t, 1], zs_s.at[t, 2])

time: 42.4 us -> 41.5 us (0.979)
  Pallas kernels: 41.6 us -> 40.5 us
    pallas_call x1, Pallas kernels: 41.6 us -> 40.5 us  [on_device(): pl.pallas_call(kernel, out_shape=pltpu.VMEM((1, LEV, ROWS, NLON), F32), i...]
where the time goes in v5:
time: 41.5 us; the launch traced here: 41.3 us
  Pallas kernels  40.5 us (98%)
  other arithmetic  0.75 us (2%)
    pallas_call x1, Pallas kernels, on_device(): pl.pallas_call(kernel, out_shape=pltpu.VMEM((1, LEV, ROWS, NLON), F32), i...  40.5 us

profile of v5, /device:TPU:8, one launch (start us, length us, event | category | flops | bytes accessed | tf_op | source)
XLA Modules:
  0.0 41.3 jit_solution(6822850273830759424)
XLA Ops:
  0.0 40.5 %shard_map.46 = f32[1,2,48,1536]{3,2,1,0:T(8,128)S(1)} custom-call(bf16[1,2,48,1536]{3,2,1,0:T(8,128)(2,1)} %prior_ref.1, bf16[1,2,48,1536]{3,2,1,0:T(8,128)(2,1)} %analysis_ref.1, f32[2,48,1536]{2,1,0:T(8,128)} %inc_ref.1, s32[2]{0:T(128)} %trunc_ref.1), custom_call_target="tpu_custom_call" | custom-call | tf_op jit(solution)/shard_map/pallas_call | solution.py:464
  40.5 0.7 %convert_element_type.3 = bf16[1,2,48,1536]{3,2,1,0:T(8,128)(2,1)} convert(f32[1,2,48,1536]{3,2,1,0:T(8,128)S(1)} %shard_map.46) | non-fusion elementwise | flops 147456 | bytes 884736 | tf_op jit(solution)/shard_map/convert_element_type | solution.py:502

commit v6 on v5

--- a/solution.py
+++ b/solution.py
@@ -20,7 +20,8 @@
 MEMBERS = NX * NZ
 QUARTER = LEV * ROWS // NX
 R = 8
-DIRECT = 6
+COMBINED = (5, 6, 7, 8)
+LAGP = 3
 AT = 6
 EARLY = 5
 WIDTH = 512
@@ -228,7 +229,7 @@
             for block in range(NZ):
                 zs[t, block, field] = total[:, block * PIECE : (block + 1) * PIECE]
 
-        if t < DIRECT:
+        if t not in COMBINED:
             for d in (2, 1, 3):
                 to = at_z(d)
                 send(zs.at[t, to], zr.at[t, z], zs_s.at[t, d], zr_s.at[t, z], (x * NZ + to, band))
@@ -254,7 +255,7 @@
             )
 
     def pass_on(t):
-        if t < DIRECT:
+        if t not in COMBINED:
             return
 
         @pl.when(middle)
@@ -268,7 +269,7 @@
                 )
 
     def spread_factors(t):
-        if t < DIRECT:
+        if t not in COMBINED:
             total = zs[t, z]
             for d in (1, 3, 2):
                 arrived(zr.at[t, at_z(d)], zr_s.at[t, at_z(d)])
@@ -385,21 +386,22 @@
     spread_sums(1)
     lax.fori_loop(40, 48, inverse_rows, 0)
     spread_sums(2)
-    pass_on(0)
     lax.fori_loop(48, 56, inverse_rows, 0)
     spread_sums(3)
-    pass_on(1)
+    for t in range(4 - LAGP):
+        pass_on(t)
     lax.fori_loop(56, inverse_steps, inverse_rows, 0)
     pl.semaphore_wait(reach.at[2], 1)
     for t in range(4, T):
         spread_sums(t)
-        pass_on(t - 2)
+        pass_on(t - LAGP)
         if t == AT:
             swap()
         if t == T - 1:
             spread_factors(0)
             spread_factors(1)
-    pass_on(T - 2)
+    for t in range(T - LAGP, T - 1):
+        pass_on(t)
     spread_factors(2)
     pass_on(T - 1)
     for t in range(3, EARLY):
@@ -439,19 +441,19 @@
         left(kp.at[group_of(d) // NZ], ks_s.at[d])
     left(ps.at[1], cs_s.at[0])
 
-    for t in range(DIRECT):
+    for t in range(T - len(COMBINED)):
         for d in (1, 2, 3):
             left(zs.at[t, at_z(d)], zs_s.at[t, d])
 
     @pl.when(end)
     def _():
-        for t in range(DIRECT, T):
+        for t in COMBINED:
             left(zs.at[t, pl.ds(jnp.where(z == 0, 2, 0), 2)], zs_s.at[t, 0])
             left(zs.at[t, beyond], zs_s.at[t, 1])
 
     @pl.when(middle)
     def _():
-        for t in range(DIRECT, T):
+        for t in COMBINED:
             left(zs.at[t, beyond], zs_s.at[t, 0])
             left(zc.at[t, 0], zs_s.at[t, 1])
             left(zc.at[t, 1], zs_s.at[t, 2])

time: 41.5 us -> 41.2 us (level)
  no operation moved by 1% of the time
where the time goes in v6:
time: 41.2 us; the launch traced here: 41 us
  Pallas kernels  40.3 us (98%)
  other arithmetic  0.75 us (2%)
    pallas_call x1, Pallas kernels, on_device(): pl.pallas_call(kernel, out_shape=pltpu.VMEM((1, LEV, ROWS, NLON), F32), i...  40.3 us

profile of v6, /device:TPU:8, one launch (start us, length us, event | category | flops | bytes accessed | tf_op | source)
XLA Modules:
  0.0 41.0 jit_solution(11867273632761678407)
XLA Ops:
  0.0 40.3 %shard_map.46 = f32[1,2,48,1536]{3,2,1,0:T(8,128)S(1)} custom-call(bf16[1,2,48,1536]{3,2,1,0:T(8,128)(2,1)} %prior_ref.1, bf16[1,2,48,1536]{3,2,1,0:T(8,128)(2,1)} %analysis_ref.1, f32[2,48,1536]{2,1,0:T(8,128)} %inc_ref.1, s32[2]{0:T(128)} %trunc_ref.1), custom_call_target="tpu_custom_call" | custom-call | tf_op jit(solution)/shard_map/pallas_call | solution.py:466
  40.3 0.7 %convert_element_type.3 = bf16[1,2,48,1536]{3,2,1,0:T(8,128)(2,1)} convert(f32[1,2,48,1536]{3,2,1,0:T(8,128)S(1)} %shard_map.46) | non-fusion elementwise | flops 147456 | bytes 884736 | tf_op jit(solution)/shard_map/convert_element_type | solution.py:504
